TPU v7x, 256 devices: a whole 4x4x8 slice. The times are simulated.
256 devices in a mesh: table: 4 (over z_lo), row: 64 (over z_hi, y, x, core).
Axes of the slice: x: 4, y: 4, z: 8 (z_hi: 2, z_lo: 4; z = z_hi * 4 + z_lo), core: 2. Of those that a mesh axis runs over, the one named last changes fastest.
Arguments:
- tables: bfloat16 [4, 524288, 128], P('table', 'row'), may hold values from -3 to 3
- indices: int32 [4, 100, 512], P('table'), may hold values from 0 to 524287
- weights: bfloat16 [4, 100, 512], P('table'), may hold values from 0.19921875 to 1
- lengths: int32 [4, 512], P('table'), may hold values from 1 to 100, as said below
Outputs:
- pooled: bfloat16 [4, 512, 128], P(None, ('table', 'row'))
Inputs may be any that keep to these rules, and one draw needn't show every extreme that they name: `lengths`: the longest bag of each table has a power of two of at most 64 positions, or 100 positions, and some table has a bag of 100.
All inputs are finite; a program needn't handle non-finite values.
Results may differ from a plain program's by a relative error of at most 0.001.
Values may be sent and summed in bfloat16 or wider, within the bound.
No kernel may reach another device: no remote copies, remote signals or barrier semaphores. Data moves between devices by JAX's collectives and lax.ppermute only.
A program may use at most 64 MiB of HBM per device.

v0:
```python
import functools

import jax
import jax.numpy as jnp
from jax import lax
from jax.experimental import pallas as pl
from jax.experimental.pallas import tpu as pltpu
from jax.sharding import Mesh
from jax.sharding import PartitionSpec as P

lanes = 128
packed_rows = 16
slots = 16
weight_unit = 1024
far_pair = 26
vmem_bytes = 20 * 2**20


def read_positions(start_ref, index_ref, weight_ref, length_ref, rank_ref, code_ref, rows):
    bag, _, batch = index_ref.shape
    padded = rank_ref.shape[0]
    local = index_ref[:, 0, :] - start_ref[0]
    position = lax.broadcasted_iota(jnp.int32, (bag, batch), 0)
    inside = (local >= 0) & (local < rows) & (position < length_ref[...])
    code = local.astype(jnp.float32) * (2.0 * weight_unit)
    code = code + weight_ref[...].astype(jnp.float32) * weight_unit
    code_ref[:bag, :] = jnp.where(inside, code, 0.0)
    code_ref[bag:, :] = jnp.zeros((padded - bag, batch), jnp.float32)

    used = jnp.where(inside, 1.0, 0.0)
    used = jnp.concatenate([used, jnp.zeros((lanes - bag, batch), jnp.float32)], 0)
    before = lax.broadcasted_iota(jnp.int32, (padded, lanes), 0) > lax.broadcasted_iota(
        jnp.int32, (padded, lanes), 1
    )
    rank = jnp.dot(
        jnp.where(before, 1.0, 0.0).astype(jnp.bfloat16),
        used.astype(jnp.bfloat16),
        preferred_element_type=jnp.float32,
    )
    rank_ref[...] = rank
    return jnp.max(rank[padded - 1 :, :], keepdims=True)


def rounds_for(most):
    return (jnp.max(most).astype(jnp.int32) + (slots - 1)) // slots


def note_repeats(plane, repeated_ref):
    row = (plane.astype(jnp.int32) // (2 * weight_unit)).astype(jnp.float32)
    slot = lax.broadcasted_iota(jnp.int32, plane.shape, 0).astype(jnp.float32)
    row = jnp.where(plane > 0, row, -1.0 - slot)
    noted = []
    for first in range(0, plane.shape[0], slots):
        rows = row[first : first + slots]
        again = jnp.full(rows.shape, -1.0, jnp.float32)
        for shift in range(1, slots // 2 + 1):
            again = jnp.where(rows == pltpu.roll(rows, shift, 0), rows, again)
        noted.append((again.astype(jnp.int32) >> 8).astype(jnp.float32))
    for pair in range(repeated_ref.shape[0]):
        repeated_ref[pair : pair + 1, :] = any_in_pair(noted, pair)


def any_in_pair(noted, pair):
    hits = [jnp.where(pairs == float(pair), 1.0, 0.0) for pairs in noted]
    return jnp.max(functools.reduce(jnp.maximum, hits), axis=0, keepdims=True)


def note_later(plane, repeated_ref):
    pairs = (plane.astype(jnp.int32) // (2 * weight_unit)) >> 8
    noted = [jnp.where(plane > 0, pairs.astype(jnp.float32), -1.0)]
    for pair in range(repeated_ref.shape[0]):
        where = slice(pair, pair + 1)
        repeated_ref[where, :] = jnp.maximum(repeated_ref[where, :], any_in_pair(noted, pair))


def fill_slots(rank_ref, code_ref, slot_refs, first, note=None, repeated_ref=None):
    high_ref, low_ref, factor_ref = slot_refs
    groups = high_ref.shape[0]
    planes = []
    for block in range(rank_ref.shape[1] // lanes):
        where = pl.ds(block * lanes, lanes)
        rank = rank_ref[:, where]
        code = code_ref[:, where]
        for s in range(slots):
            at = rank == (first + s).astype(jnp.float32)
            planes.append(jnp.sum(jnp.where(at, code, 0.0), axis=0, keepdims=True))
    plane = jnp.concatenate(planes, 0)
    if note is not None:
        note(plane, repeated_ref)
    plane = jnp.concatenate([plane, pltpu.roll(plane, lanes - groups, 1)], 0)
    low_ref[...] = (plane.astype(jnp.int32) // (2 * weight_unit) % lanes).astype(jnp.float32)
    code = plane.T[:groups].astype(jnp.int32)
    row = code // (2 * weight_unit)
    high_ref[...] = (row // lanes).astype(jnp.float32)
    factor = (code % (2 * weight_unit)).astype(jnp.float32)
    factor_ref[...] = factor * (1.0 / weight_unit)


def spread_half(slot_refs, spread_ref, core, tiles, add):
    high_ref, low_ref, factor_ref = slot_refs
    group_bags = lanes // slots
    half_groups = high_ref.shape[0] // 2
    stride = spread_ref.shape[0] // tiles
    row_id = lax.broadcasted_iota(jnp.int32, (packed_rows, lanes), 0)
    row_ids = [
        (row_id + packed_rows * i).astype(jnp.float32).astype(jnp.bfloat16)
        for i in range(tiles // packed_rows)
    ]
    zero = jnp.zeros((packed_rows, lanes), jnp.bfloat16)
    lane = lax.broadcasted_iota(jnp.int32, (lanes, lanes), 1).astype(jnp.float32)
    lows = pltpu.roll(low_ref[...], (lanes - 2 * core) % lanes, 1)
    owner = lax.broadcasted_iota(jnp.int32, (packed_rows, lanes), 1) // slots
    owner = owner.astype(jnp.float32).astype(jnp.bfloat16)
    owned = [owner == jnp.full_like(owner, g) for g in range(group_bags)]

    def row_of(ref, j):
        row = ref[pl.ds(j, 1), :]
        return jnp.broadcast_to(row, (packed_rows, lanes)).astype(jnp.bfloat16)

    def spread_group(t):
        j = t // 2 * 4 + t % 2 + 2 * core
        high = row_of(high_ref, j)
        factor = row_of(factor_ref, j)
        at = [high == ids for ids in row_ids]
        by_high = []
        for g in range(group_bags):
            mine = jnp.where(owned[g], factor, zero)
            by_high += [jnp.where(hit, mine, zero) for hit in at]
        at_lane = t // 2 * 4 + t % 2
        low = jnp.broadcast_to(lows[:, at_lane : at_lane + 1], (lanes, lanes))
        by_low = jnp.where(low == lane, 1.0, 0.0).astype(jnp.bfloat16)
        total = lax.dot_general(
            jnp.concatenate(by_high, 0),
            by_low,
            (((1,), (0,)), ((), ())),
            preferred_element_type=jnp.float32,
        )
        blocks = group_bags // 2
        for g in range(group_bags):
            pair = (g // blocks * half_groups + t) // 2 ^ far_pair
            bag = g % blocks * 2 * half_groups + pair * 2 + t % 2
            where = pl.ds(bag, tiles, stride=stride)
            part = total[g * tiles : (g + 1) * tiles]
            if add:
                part = part + spread_ref[where, :]
            spread_ref[where, :] = part

    numbers = range(half_groups)
    if add:
        found = [jnp.max(factor_ref[pl.ds(t // 2 * 4 + t % 2 + 2 * core, 1), :]) for t in numbers]
        for t in numbers:
            pl.when(found[t] > 0)(functools.partial(spread_group, t))
    else:
        for t in numbers:
            spread_group(t)


def multiply(spread_ref, table_ref, repeated_ref, core, out_ref):
    tiles = table_ref.shape[0] // lanes
    stride = spread_ref.shape[0] // tiles
    bags = out_ref.shape[0]
    lane = lax.broadcasted_iota(jnp.int32, (1, lanes), 1)
    ours = (lane // 2) % 2 == core
    left = [
        jnp.where(ours, repeated_ref[pair : pair + 1, :], 0.0) for pair in range(tiles // 2)
    ]
    any_left = jnp.max(functools.reduce(jnp.maximum, left)) > 0
    left = [jnp.max(some) > 0 for some in left]
    factors = [
        spread_ref[pl.ds(i * stride, bags), :].astype(jnp.bfloat16) for i in range(tiles)
    ]
    out_ref[...] = jnp.dot(
        jnp.concatenate(factors, 1), table_ref[...], preferred_element_type=jnp.float32
    )

    def add_rest(pair):
        factors = [spread_ref[pl.ds((2 * pair + i) * stride, bags), :] for i in range(2)]
        factors = jnp.concatenate(factors, 1)
        rest = factors - factors.astype(jnp.bfloat16).astype(jnp.float32)
        out_ref[...] += jnp.dot(
            rest.astype(jnp.bfloat16),
            table_ref[pl.ds(2 * pair * lanes, 2 * lanes), :],
            preferred_element_type=jnp.float32,
        )

    @pl.when(any_left)
    def _():
        for pair in range(tiles // 2):
            pl.when(left[pair])(functools.partial(add_rest, pair))


def send_kernel(
    start_ref,
    core_ref,
    index_hbm,
    weight_hbm,
    length_hbm,
    table_hbm,
    out_ref,
    high_ref,
    low_ref,
    factor_ref,
    most_ref,
    repeated_ref,
    rank_ref,
    code_ref,
    table_ref,
    index_ref,
    weight_ref,
    length_ref,
    high_later,
    low_later,
    factor_later,
    spread_ref,
    table_sem,
    index_sem,
    weight_sem,
    length_sem,
):
    copies = [
        pltpu.make_async_copy(index_hbm, index_ref, index_sem),
        pltpu.make_async_copy(weight_hbm, weight_ref, weight_sem),
        pltpu.make_async_copy(length_hbm, length_ref, length_sem),
    ]
    for copy in copies:
        copy.start()
    for copy in copies:
        copy.wait()
    table_copy = pltpu.make_async_copy(table_hbm, table_ref, table_sem)
    table_copy.start()
    rows = table_ref.shape[0]
    tiles = rows // lanes
    core = 1 - core_ref[0]
    most = read_positions(
        start_ref, index_ref, weight_ref, length_ref, rank_ref, code_ref, rows
    )
    most_ref[...] = jnp.broadcast_to(most, most_ref.shape)
    rounds = rounds_for(most)
    slot_refs = (high_ref, low_ref, factor_ref)
    later_refs = (high_later, low_later, factor_later)
    fill_slots(rank_ref, code_ref, slot_refs, jnp.int32(0), note_repeats, repeated_ref)
    spread_half(slot_refs, spread_ref, core, tiles, False)

    def later_round(number, carry):
        fill_slots(rank_ref, code_ref, later_refs, number * slots, note_later, repeated_ref)
        spread_half(later_refs, spread_ref, core, tiles, True)
        return carry

    lax.fori_loop(1, rounds, later_round, 0)
    table_copy.wait()
    multiply(spread_ref, table_ref, repeated_ref, core, out_ref)


def keep_kernel(
    start_ref,
    core_ref,
    most_ref,
    repeated_ref,
    rank_ref,
    code_ref,
    high_ref,
    low_ref,
    factor_ref,
    table_hbm,
    out_ref,
    table_ref,
    high_later,
    low_later,
    factor_later,
    spread_ref,
    table_sem,
):
    table_copy = pltpu.make_async_copy(table_hbm, table_ref, table_sem)
    table_copy.start()
    rows = table_ref.shape[0]
    tiles = rows // lanes
    core = core_ref[0]
    slot_refs = (high_ref, low_ref, factor_ref)
    later_refs = (high_later, low_later, factor_later)
    spread_half(slot_refs, spread_ref, core, tiles, False)
    rounds = rounds_for(most_ref[...])

    def later_round(number, carry):
        fill_slots(rank_ref, code_ref, later_refs, number * slots)
        spread_half(later_refs, spread_ref, core, tiles, True)
        return carry

    lax.fori_loop(1, rounds, later_round, 0)
    table_copy.wait()
    multiply(spread_ref, table_ref, repeated_ref, core, out_ref)


def kernels(table_rows, index_rows, weight, length, row_start, core):
    rows, width = table_rows.shape
    bag, batch = weight.shape
    padded = bag + 8 - bag % 8
    groups = batch * slots // lanes
    half = batch // 2
    tiles = rows // lanes
    smem = pl.BlockSpec(memory_space=pltpu.SMEM)
    vmem = pl.BlockSpec(memory_space=pltpu.VMEM)
    far = pl.BlockSpec(memory_space=pl.ANY)
    table_scratch = pltpu.VMEM((rows, width), table_rows.dtype)
    by_position = jax.ShapeDtypeStruct((padded, batch), jnp.float32)
    by_group = [pltpu.VMEM((n, lanes), jnp.float32) for n in (groups, lanes, groups)]
    spread = pltpu.VMEM(((half + 1) * tiles, lanes), jnp.float32)
    dma = pltpu.SemaphoreType.DMA
    scratch = [
        table_scratch,
        pltpu.VMEM(index_rows.shape, index_rows.dtype),
        pltpu.VMEM(weight.shape, weight.dtype),
        pltpu.VMEM(length.shape, length.dtype),
        *by_group,
        spread,
        dma,
        dma,
        dma,
        dma,
    ]
    limit = pltpu.CompilerParams(vmem_limit_bytes=vmem_bytes)
    index_rows, weight, length, table_rows = [
        pltpu.with_memory_space_constraint(value, pltpu.HBM)
        for value in (index_rows, weight, length, table_rows)
    ]
    pools = jax.ShapeDtypeStruct((half, width), jnp.float32)
    slot = [jax.ShapeDtypeStruct((n, lanes), jnp.float32) for n in (groups, lanes, groups)]
    place = (row_start.reshape(1), core.reshape(1))

    sent, high, low, factor, most, repeated, rank, code = pl.pallas_call(
        send_kernel,
        out_shape=(
            pools,
            *slot,
            jax.ShapeDtypeStruct((8, lanes), jnp.float32),
            jax.ShapeDtypeStruct((tiles // 2, lanes), jnp.float32),
            by_position,
            by_position,
        ),
        in_specs=[smem, smem, far, far, far, far],
        out_specs=(vmem,) * 8,
        scratch_shapes=scratch,
        compiler_params=limit,
    )(*place, index_rows, weight, length, table_rows)

    def keep():
        return pl.pallas_call(
            keep_kernel,
            out_shape=pools,
            in_specs=[smem, smem, vmem, vmem, vmem, vmem, vmem, vmem, vmem, far],
            out_specs=vmem,
            scratch_shapes=[table_scratch, *by_group, spread, dma],
            compiler_params=limit,
            cost_estimate=pl.CostEstimate(
                flops=8 * half * rows * width, bytes_accessed=rows * width * 2, transcendentals=0
            ),
        )(*place, most, repeated, rank, code, high, low, factor, table_rows)

    return sent, keep


def on_device(tables, indices, weights, lengths):
    _, row_dev, feature_width = tables.shape
    batch_size = indices.shape[2]
    table_count = lax.axis_size("table")
    pair_count = lax.axis_size("pair")
    core = lax.axis_index("core").astype(jnp.int32)
    row = lax.axis_index("pair").astype(jnp.int32) * 2 + core
    index_rows = indices.transpose(1, 0, 2)
    sent, keep = kernels(tables[0], index_rows, weights[0], lengths, row * row_dev, core)
    received = lax.ppermute(sent, "core", [(0, 1), (1, 0)])
    partial = keep() + received
    share = batch_size // (table_count * pair_count * 2)
    tiles = partial.reshape(table_count * pair_count, share, feature_width)
    groups = [
        [(t * pair_count + (p ^ far_pair)) * 2 + c for t in range(table_count) for p in range(pair_count)]
        for c in range(2)
    ]
    arrived = lax.all_to_all(
        tiles,
        ("table", "pair", "core"),
        split_axis=0,
        concat_axis=0,
        axis_index_groups=groups,
        tiled=True,
    )
    shares = arrived.reshape(table_count, pair_count, share, feature_width)
    return shares.sum(axis=1).astype(jnp.bfloat16)


def solution(mesh):
    tables, rows = mesh.devices.shape
    by_core = Mesh(mesh.devices.reshape(tables, rows // 2, 2), ("table", "pair", "core"))
    row = ("pair", "core")
    placed = (
        P("table", row, None),
        P("table", None, None),
        P("table", None, None),
        P("table", None),
    )
    return jax.shard_map(
        on_device,
        mesh=by_core,
        in_specs=placed,
        out_specs=P(None, ("table", *row), None),
        check_vma=False,
    )
```

profile of v0, /device:TPU:1, one launch (start us, length us, event | category | flops | bytes accessed | tf_op | source)
XLA Modules:
  0.0 31.5 jit_solution(9046978631663944623)
XLA Ops:
  0.0 4.7 %shard_map.46 = (f32[256,128]{1,0:T(8,128)S(1)}, f32[64,128]{1,0:T(8,128)S(1)}, f32[128,128]{1,0:T(8,128)S(1)}, f32[64,128]{1,0:T(8,128)S(1)}, f32[8,128]{1,0:T(...) custom-call(s32[1]{0:T(128)} %bitcast.start_ref, s32[1]{0:T(128)} %bitcast.1.core_ref, ...), custom_call_target="tpu_custom_call" | custom-call | tf_op jit(solution)/shard_map/pallas_call | solution.py:329
  4.7 3.6 %collective-permute-start = (f32[256,128]{1,0:T(8,128)S(1)}, f32[256,128]{1,0:T(8,128)S(1)}, u32[]{:S(2)}, u32[]{:S(2)}) collective-permute-start(f32[256,128]{1,0:T(8,128)S(1)} %get-tuple-element.20), channel_id=1, source_target_pairs={{0,1},{1,0},{2,3},{3,2},{4,5},{5,4},{6,7},{7,6},{8,9},{9,8},{10,11... | collective-permute-start | bytes 393224 | tf_op jit(solution)/shard_map/ppermute | solution.py:370
  8.3 3.2 %shard_map.47 = f32[256,128]{1,0:T(8,128)S(1)} custom-call(s32[1]{0:T(128)} %bitcast.start_ref, s32[1]{0:T(128)} %bitcast.1.core_ref, f32[8,128]{1,0:T(8,128)S(1)} %get-tuple-element.13.most_ref, f32[32,128]{1,0:T(8,128)S(1)} %get-tuple-element.14.repeated_ref, f32[104,512]{1,0:T(8,128)S(1)} %get-tuple-element.15.rank_ref, ...), custom_call_target="tpu_custom_call" | custom-call | flops 2147483648 | bytes 2097152 | tf_op jit(solution)/shard_map/pallas_call | solution.py:346
  11.6 0.0 collective-permute-done
  11.6 19.2 %all_to_all.5 = f32[128,2,128]{2,1,0:T(2,128)S(1)} all-to-all(f32[128,2,128]{2,1,0:T(2,128)S(1)} %bitcast.10), channel_id=1, replica_groups={{52,54,48,50,60,62,56,58,36,38,32,34,44,46,40,42,20,22,16,18,28,30,24,2..., dimensions={0} | all-to-all | bytes 262144 | tf_op jit(solution)/shard_map/all_to_all | solution.py:378
  30.8 0.6 %bitcast_reduce_fusion = bf16[4,2,128]{2,1,0:T(2,128)(2,1)} fusion(f32[128,2,128]{2,1,0:T(2,128)S(1)} %all_to_all.5), kind=kLoop, calls=%fused_computation | loop fusion | flops 31744 | bytes 133120 | tf_op jit(solution)/shard_map/reduce_sum | solution.py:387
  (1 shorter events, 0.0 us)
Async XLA Ops:
  4.7 6.9 %collective-permute-start = (f32[256,128]{1,0:T(8,128)S(1)}, f32[256,128]{1,0:T(8,128)S(1)}, u32[]{:S(2)}, u32[]{:S(2)}) collective-permute-start(f32[256,128]{1,0:T(8,128)S(1)} %get-tuple-element.20), channel_id=1, source_target_pairs={{0,1},{1,0},{2,3},{3,2},{4,5},{5,4},{6,7},{7,6},{8,9},{9,8},{10,11... | collective-permute-start | bytes 393224 | tf_op jit(solution)/shard_map/ppermute | solution.py:370
where the time goes:
time: 31.5 us
  blocking collectives  19.2 us (61%)
  Pallas kernels  7.92 us (25%)
  starting transfers between devices  3.62 us (11%)
  other arithmetic  0.64 us (2%)
    all_to_all x1, blocking collectives, on_device(): lax.all_to_all(tiles, ('table', 'pair', 'core'), split_axis=0, concat_axi...  19.2 us
    pallas_call x1, Pallas kernels, kernels(): pl.pallas_call(send_kernel, out_shape=(pools, *slot, jax.ShapeDtypeStruct...  4.69 us
    ppermute x1, starting transfers between devices, on_device(): received = lax.ppermute(sent, 'core', [(0, 1), (1, 0)])  3.62 us
    pallas_call x1, Pallas kernels, keep(): pl.pallas_call(keep_kernel, out_shape=pools, in_specs=[smem, smem, vmem,...  3.23 us
  transfers between devices with their start and end apart: 1, of which 0 were waited for; matrix products, arithmetic and copies ran while one was open for 0% of the time, Pallas kernels for 10%

commit v1 on v0

--- a/solution.py
+++ b/solution.py
@@ -17,9 +17,10 @@
 
 
 def read_positions(start_ref, index_ref, weight_ref, length_ref, rank_ref, code_ref, rows):
-    bag, _, batch = index_ref.shape
+    bag, batch = weight_ref.shape
     padded = rank_ref.shape[0]
-    local = index_ref[:, 0, :] - start_ref[0]
+    blocks = [index_ref[block, :, 0, :] for block in range(batch // lanes)]
+    local = jnp.concatenate(blocks, 1) - start_ref[0]
     position = lax.broadcasted_iota(jnp.int32, (bag, batch), 0)
     inside = (local >= 0) & (local < rows) & (position < length_ref[...])
     code = local.astype(jnp.float32) * (2.0 * weight_unit)
@@ -73,7 +74,7 @@
         repeated_ref[where, :] = jnp.maximum(repeated_ref[where, :], any_in_pair(noted, pair))
 
 
-def fill_slots(rank_ref, code_ref, slot_refs, first, note=None, repeated_ref=None):
+def fill_slots(rank_ref, code_ref, slot_refs, first):
     high_ref, low_ref, factor_ref = slot_refs
     groups = high_ref.shape[0]
     planes = []
@@ -84,16 +85,15 @@
         for s in range(slots):
             at = rank == (first + s).astype(jnp.float32)
             planes.append(jnp.sum(jnp.where(at, code, 0.0), axis=0, keepdims=True))
-    plane = jnp.concatenate(planes, 0)
-    if note is not None:
-        note(plane, repeated_ref)
-    plane = jnp.concatenate([plane, pltpu.roll(plane, lanes - groups, 1)], 0)
+    slot_codes = jnp.concatenate(planes, 0)
+    plane = jnp.concatenate([slot_codes, pltpu.roll(slot_codes, lanes - groups, 1)], 0)
     low_ref[...] = (plane.astype(jnp.int32) // (2 * weight_unit) % lanes).astype(jnp.float32)
     code = plane.T[:groups].astype(jnp.int32)
     row = code // (2 * weight_unit)
     high_ref[...] = (row // lanes).astype(jnp.float32)
     factor = (code % (2 * weight_unit)).astype(jnp.float32)
     factor_ref[...] = factor * (1.0 / weight_unit)
+    return slot_codes
 
 
 def spread_half(slot_refs, spread_ref, core, tiles, add):
@@ -218,7 +218,14 @@
     length_sem,
 ):
     copies = [
-        pltpu.make_async_copy(index_hbm, index_ref, index_sem),
+        *[
+            pltpu.make_async_copy(
+                index_hbm.at[:, :, pl.ds(block * lanes, lanes)],
+                index_ref.at[block],
+                index_sem.at[block],
+            )
+            for block in range(index_ref.shape[0])
+        ],
         pltpu.make_async_copy(weight_hbm, weight_ref, weight_sem),
         pltpu.make_async_copy(length_hbm, length_ref, length_sem),
     ]
@@ -238,11 +245,12 @@
     rounds = rounds_for(most)
     slot_refs = (high_ref, low_ref, factor_ref)
     later_refs = (high_later, low_later, factor_later)
-    fill_slots(rank_ref, code_ref, slot_refs, jnp.int32(0), note_repeats, repeated_ref)
+    plane = fill_slots(rank_ref, code_ref, slot_refs, jnp.int32(0))
     spread_half(slot_refs, spread_ref, core, tiles, False)
+    note_repeats(plane, repeated_ref)
 
     def later_round(number, carry):
-        fill_slots(rank_ref, code_ref, later_refs, number * slots, note_later, repeated_ref)
+        note_later(fill_slots(rank_ref, code_ref, later_refs, number * slots), repeated_ref)
         spread_half(later_refs, spread_ref, core, tiles, True)
         return carry
 
@@ -261,17 +269,13 @@
     high_ref,
     low_ref,
     factor_ref,
-    table_hbm,
+    table_ref,
     out_ref,
-    table_ref,
     high_later,
     low_later,
     factor_later,
     spread_ref,
-    table_sem,
 ):
-    table_copy = pltpu.make_async_copy(table_hbm, table_ref, table_sem)
-    table_copy.start()
     rows = table_ref.shape[0]
     tiles = rows // lanes
     core = core_ref[0]
@@ -286,7 +290,6 @@
         return carry
 
     lax.fori_loop(1, rounds, later_round, 0)
-    table_copy.wait()
     multiply(spread_ref, table_ref, repeated_ref, core, out_ref)
 
 
@@ -300,20 +303,18 @@
     smem = pl.BlockSpec(memory_space=pltpu.SMEM)
     vmem = pl.BlockSpec(memory_space=pltpu.VMEM)
     far = pl.BlockSpec(memory_space=pl.ANY)
-    table_scratch = pltpu.VMEM((rows, width), table_rows.dtype)
     by_position = jax.ShapeDtypeStruct((padded, batch), jnp.float32)
     by_group = [pltpu.VMEM((n, lanes), jnp.float32) for n in (groups, lanes, groups)]
     spread = pltpu.VMEM(((half + 1) * tiles, lanes), jnp.float32)
     dma = pltpu.SemaphoreType.DMA
     scratch = [
-        table_scratch,
-        pltpu.VMEM(index_rows.shape, index_rows.dtype),
+        pltpu.VMEM((batch // lanes, bag, 1, lanes), index_rows.dtype),
         pltpu.VMEM(weight.shape, weight.dtype),
         pltpu.VMEM(length.shape, length.dtype),
         *by_group,
         spread,
         dma,
-        dma,
+        dma((batch // lanes,)),
         dma,
         dma,
     ]
@@ -326,7 +327,7 @@
     slot = [jax.ShapeDtypeStruct((n, lanes), jnp.float32) for n in (groups, lanes, groups)]
     place = (row_start.reshape(1), core.reshape(1))
 
-    sent, high, low, factor, most, repeated, rank, code = pl.pallas_call(
+    sent, high, low, factor, most, repeated, rank, code, table = pl.pallas_call(
         send_kernel,
         out_shape=(
             pools,
@@ -335,9 +336,10 @@
             jax.ShapeDtypeStruct((tiles // 2, lanes), jnp.float32),
             by_position,
             by_position,
+            jax.ShapeDtypeStruct(table_rows.shape, table_rows.dtype),
         ),
         in_specs=[smem, smem, far, far, far, far],
-        out_specs=(vmem,) * 8,
+        out_specs=(vmem,) * 9,
         scratch_shapes=scratch,
         compiler_params=limit,
     )(*place, index_rows, weight, length, table_rows)
@@ -346,14 +348,14 @@
         return pl.pallas_call(
             keep_kernel,
             out_shape=pools,
-            in_specs=[smem, smem, vmem, vmem, vmem, vmem, vmem, vmem, vmem, far],
+            in_specs=[smem, smem, *[vmem] * 8],
             out_specs=vmem,
-            scratch_shapes=[table_scratch, *by_group, spread, dma],
+            scratch_shapes=[*by_group, spread],
             compiler_params=limit,
             cost_estimate=pl.CostEstimate(
                 flops=8 * half * rows * width, bytes_accessed=rows * width * 2, transcendentals=0
             ),
-        )(*place, most, repeated, rank, code, high, low, factor, table_rows)
+        )(*place, most, repeated, rank, code, high, low, factor, table)
 
     return sent, keep
 

time: 31.5 us -> 31.9 us (1.013)
  blocking collectives: 19.2 us -> 20.3 us
  starting transfers between devices: 3.62 us -> 3.29 us
    all_to_all x1, blocking collectives: 19.2 us -> 20.3 us  [on_device(): lax.all_to_all(tiles, ('table', 'pair', 'core'), split_axis=0, concat_axi...]
    ppermute x1, starting transfers between devices: 3.62 us -> 3.29 us  [on_device(): received = lax.ppermute(sent, 'core', [(0, 1), (1, 0)])]
  transfers between devices with their start and end apart: 1 -> 1, of which waited for: 0 -> 0; matrix products, arithmetic and copies ran while one was open for 0% -> 0% of each run, Pallas kernels for 10% -> 9%
where the time goes in v1:
time: 31.9 us; the launch traced here: 32 us
  blocking collectives  20.3 us (64%)
  Pallas kernels  7.73 us (24%)
  starting transfers between devices  3.29 us (10%)
  other arithmetic  0.64 us (2%)
    all_to_all x1, blocking collectives, on_device(): lax.all_to_all(tiles, ('table', 'pair', 'core'), split_axis=0, concat_axi...  20.3 us
    pallas_call x1, Pallas kernels, kernels(): pl.pallas_call(send_kernel, out_shape=(pools, *slot, jax.ShapeDtypeStruct...  4.8 us
    ppermute x1, starting transfers between devices, on_device(): received = lax.ppermute(sent, 'core', [(0, 1), (1, 0)])  3.29 us
    pallas_call x1, Pallas kernels, keep(): pl.pallas_call(keep_kernel, out_shape=pools, in_specs=[smem, smem, *[vmem...  2.93 us
  transfers between devices with their start and end apart: 1, of which 0 were waited for; matrix products, arithmetic and copies ran while one was open for 0% of the time, Pallas kernels for 9%

profile of v1, /device:TPU:1, one launch (start us, length us, event | category | flops | bytes accessed | tf_op | source)
XLA Modules:
  0.0 32.0 jit_solution(7432478930240825241)
XLA Ops:
  0.0 4.8 %shard_map.46 = (f32[256,128]{1,0:T(8,128)S(1)}, f32[64,128]{1,0:T(8,128)S(1)}, f32[128,128]{1,0:T(8,128)S(1)}, f32[64,128]{1,0:T(8,128)S(1)}, f32[8,128]{1,0:T(...) custom-call(s32[1]{0:T(128)} %bitcast.start_ref, ...), custom_call_target="tpu_custom_call" | custom-call | tf_op jit(solution)/shard_map/pallas_call | solution.py:330
  4.8 3.3 %collective-permute-start = (f32[256,128]{1,0:T(8,128)S(1)}, f32[256,128]{1,0:T(8,128)S(1)}, u32[]{:S(2)}, u32[]{:S(2)}) collective-permute-start(f32[256,128]{1,0:T(8,128)S(1)} %get-tuple-element.22), channel_id=1, source_target_pairs={{0,1},{1,0},{2,3},{3,2},{4,5},{5,4},{6,7},{7,6},{8,9},{9,8},{10,11... | collective-permute-start | bytes 393224 | tf_op jit(solution)/shard_map/ppermute | solution.py:372
  8.1 2.9 %shard_map.47 = f32[256,128]{1,0:T(8,128)S(1)} custom-call(s32[1]{0:T(128)} %bitcast.start_ref, s32[1]{0:T(128)} %bitcast.1.core_ref, f32[8,128]{1,0:T(8,128)S(1)} %get-tuple-element.14.most_ref, f32[32,128]{1,0:T(8,128)S(1)} %get-tuple-element.15.repeated_ref, f32[104,512]{1,0:T(8,128)S(1)} %get-tuple-element.16.rank_ref, ...), custom_call_target="tpu_custom_call" | custom-call | flops 2147483648 | bytes 2097152 | tf_op jit(solution)/shard_map/pallas_call | solution.py:348
  11.0 0.0 collective-permute-done
  11.1 20.3 %all_to_all.5 = f32[128,2,128]{2,1,0:T(2,128)S(1)} all-to-all(f32[128,2,128]{2,1,0:T(2,128)S(1)} %bitcast.9), channel_id=1, replica_groups={{52,54,48,50,60,62,56,58,36,38,32,34,44,46,40,42,20,22,16,18,28,30,24,2..., dimensions={0} | all-to-all | bytes 262144 | tf_op jit(solution)/shard_map/all_to_all | solution.py:380
  31.4 0.6 %bitcast_reduce_fusion = bf16[4,2,128]{2,1,0:T(2,128)(2,1)} fusion(f32[128,2,128]{2,1,0:T(2,128)S(1)} %all_to_all.5), kind=kLoop, calls=%fused_computation | loop fusion | flops 31744 | bytes 133120 | tf_op jit(solution)/shard_map/reduce_sum | solution.py:389
  (1 shorter events, 0.0 us)
Async XLA Ops:
  4.8 6.2 %collective-permute-start = (f32[256,128]{1,0:T(8,128)S(1)}, f32[256,128]{1,0:T(8,128)S(1)}, u32[]{:S(2)}, u32[]{:S(2)}) collective-permute-start(f32[256,128]{1,0:T(8,128)S(1)} %get-tuple-element.22), channel_id=1, source_target_pairs={{0,1},{1,0},{2,3},{3,2},{4,5},{5,4},{6,7},{7,6},{8,9},{9,8},{10,11... | collective-permute-start | bytes 393224 | tf_op jit(solution)/shard_map/ppermute | solution.py:372

commit v2 on v0

--- a/solution.py
+++ b/solution.py
@@ -74,32 +74,33 @@
 
 
 def fill_slots(rank_ref, code_ref, slot_refs, first, note=None, repeated_ref=None):
-    high_ref, low_ref, factor_ref = slot_refs
-    groups = high_ref.shape[0]
     planes = []
-    for block in range(rank_ref.shape[1] // lanes):
+    for block, (high_ref, low_ref, factor_ref) in enumerate(slot_refs):
+        rows = high_ref.shape[0]
         where = pl.ds(block * lanes, lanes)
         rank = rank_ref[:, where]
         code = code_ref[:, where]
+        filled = []
         for s in range(slots):
             at = rank == (first + s).astype(jnp.float32)
-            planes.append(jnp.sum(jnp.where(at, code, 0.0), axis=0, keepdims=True))
-    plane = jnp.concatenate(planes, 0)
+            filled.append(jnp.sum(jnp.where(at, code, 0.0), axis=0, keepdims=True))
+        plane = jnp.concatenate(filled, 0)
+        planes.append(plane)
+        shifts = [(lanes - rows * g) % lanes for g in range(lanes // rows)]
+        plane = jnp.concatenate([pltpu.roll(plane, n, 1) if n else plane for n in shifts], 0)
+        low_ref[...] = (plane.astype(jnp.int32) // (2 * weight_unit) % lanes).astype(jnp.float32)
+        code = plane.T[:rows].astype(jnp.int32)
+        row = code // (2 * weight_unit)
+        high_ref[...] = (row // lanes).astype(jnp.float32)
+        factor = (code % (2 * weight_unit)).astype(jnp.float32)
+        factor_ref[...] = factor * (1.0 / weight_unit)
     if note is not None:
-        note(plane, repeated_ref)
-    plane = jnp.concatenate([plane, pltpu.roll(plane, lanes - groups, 1)], 0)
-    low_ref[...] = (plane.astype(jnp.int32) // (2 * weight_unit) % lanes).astype(jnp.float32)
-    code = plane.T[:groups].astype(jnp.int32)
-    row = code // (2 * weight_unit)
-    high_ref[...] = (row // lanes).astype(jnp.float32)
-    factor = (code % (2 * weight_unit)).astype(jnp.float32)
-    factor_ref[...] = factor * (1.0 / weight_unit)
+        note(jnp.concatenate(planes, 0), repeated_ref)
 
 
 def spread_half(slot_refs, spread_ref, core, tiles, add):
-    high_ref, low_ref, factor_ref = slot_refs
     group_bags = lanes // slots
-    half_groups = high_ref.shape[0] // 2
+    block_groups = slots // 2
     stride = spread_ref.shape[0] // tiles
     row_id = lax.broadcasted_iota(jnp.int32, (packed_rows, lanes), 0)
     row_ids = [
@@ -108,7 +109,9 @@
     ]
     zero = jnp.zeros((packed_rows, lanes), jnp.bfloat16)
     lane = lax.broadcasted_iota(jnp.int32, (lanes, lanes), 1).astype(jnp.float32)
-    lows = pltpu.roll(low_ref[...], (lanes - 2 * core) % lanes, 1)
+    lows = [
+        pltpu.roll(low_ref[...], (lanes - 2 * core) % lanes, 1) for _, low_ref, _ in slot_refs
+    ]
     owner = lax.broadcasted_iota(jnp.int32, (packed_rows, lanes), 1) // slots
     owner = owner.astype(jnp.float32).astype(jnp.bfloat16)
     owned = [owner == jnp.full_like(owner, g) for g in range(group_bags)]
@@ -117,7 +120,8 @@
         row = ref[pl.ds(j, 1), :]
         return jnp.broadcast_to(row, (packed_rows, lanes)).astype(jnp.bfloat16)
 
-    def spread_group(t):
+    def spread_group(block, t):
+        high_ref, _, factor_ref = slot_refs[block]
         j = t // 2 * 4 + t % 2 + 2 * core
         high = row_of(high_ref, j)
         factor = row_of(factor_ref, j)
@@ -127,7 +131,7 @@
             mine = jnp.where(owned[g], factor, zero)
             by_high += [jnp.where(hit, mine, zero) for hit in at]
         at_lane = t // 2 * 4 + t % 2
-        low = jnp.broadcast_to(lows[:, at_lane : at_lane + 1], (lanes, lanes))
+        low = jnp.broadcast_to(lows[block][:, at_lane : at_lane + 1], (lanes, lanes))
         by_low = jnp.where(low == lane, 1.0, 0.0).astype(jnp.bfloat16)
         total = lax.dot_general(
             jnp.concatenate(by_high, 0),
@@ -135,24 +139,26 @@
             (((1,), (0,)), ((), ())),
             preferred_element_type=jnp.float32,
         )
-        blocks = group_bags // 2
         for g in range(group_bags):
-            pair = (g // blocks * half_groups + t) // 2 ^ far_pair
-            bag = g % blocks * 2 * half_groups + pair * 2 + t % 2
+            pair = (g * block_groups + t) // 2 ^ far_pair
+            bag = block * lanes // 2 + pair * 2 + t % 2
             where = pl.ds(bag, tiles, stride=stride)
             part = total[g * tiles : (g + 1) * tiles]
             if add:
                 part = part + spread_ref[where, :]
             spread_ref[where, :] = part
 
-    numbers = range(half_groups)
+    numbers = [(block, t) for block in range(len(slot_refs)) for t in range(block_groups)]
     if add:
-        found = [jnp.max(factor_ref[pl.ds(t // 2 * 4 + t % 2 + 2 * core, 1), :]) for t in numbers]
-        for t in numbers:
-            pl.when(found[t] > 0)(functools.partial(spread_group, t))
+        found = []
+        for block, t in numbers:
+            factors = slot_refs[block][2][pl.ds(t // 2 * 4 + t % 2 + 2 * core, 1), :]
+            found.append(jnp.max(factors))
+        for number, some in zip(numbers, found):
+            pl.when(some > 0)(functools.partial(spread_group, *number))
     else:
-        for t in numbers:
-            spread_group(t)
+        for number in numbers:
+            spread_group(*number)
 
 
 def multiply(spread_ref, table_ref, repeated_ref, core, out_ref):
@@ -189,34 +195,17 @@
             pl.when(left[pair])(functools.partial(add_rest, pair))
 
 
-def send_kernel(
-    start_ref,
-    core_ref,
-    index_hbm,
-    weight_hbm,
-    length_hbm,
-    table_hbm,
-    out_ref,
-    high_ref,
-    low_ref,
-    factor_ref,
-    most_ref,
-    repeated_ref,
-    rank_ref,
-    code_ref,
-    table_ref,
-    index_ref,
-    weight_ref,
-    length_ref,
-    high_later,
-    low_later,
-    factor_later,
-    spread_ref,
-    table_sem,
-    index_sem,
-    weight_sem,
-    length_sem,
-):
+def by_block(refs):
+    return [refs[i : i + 3] for i in range(0, len(refs), 3)]
+
+
+def send_kernel(blocks, *refs):
+    start_ref, core_ref, index_hbm, weight_hbm, length_hbm, table_hbm, *refs = refs
+    out_ref, most_ref, repeated_ref, rank_ref, code_ref, *refs = refs
+    slot_refs = by_block(refs[: 3 * blocks])
+    later_refs = by_block(refs[3 * blocks : 6 * blocks])
+    index_ref, weight_ref, length_ref, table_ref, spread_ref, *sems = refs[6 * blocks :]
+    table_sem, index_sem, weight_sem, length_sem = sems
     copies = [
         pltpu.make_async_copy(index_hbm, index_ref, index_sem),
         pltpu.make_async_copy(weight_hbm, weight_ref, weight_sem),
@@ -236,8 +225,6 @@
     )
     most_ref[...] = jnp.broadcast_to(most, most_ref.shape)
     rounds = rounds_for(most)
-    slot_refs = (high_ref, low_ref, factor_ref)
-    later_refs = (high_later, low_later, factor_later)
     fill_slots(rank_ref, code_ref, slot_refs, jnp.int32(0), note_repeats, repeated_ref)
     spread_half(slot_refs, spread_ref, core, tiles, False)
 
@@ -251,32 +238,16 @@
     multiply(spread_ref, table_ref, repeated_ref, core, out_ref)
 
 
-def keep_kernel(
-    start_ref,
-    core_ref,
-    most_ref,
-    repeated_ref,
-    rank_ref,
-    code_ref,
-    high_ref,
-    low_ref,
-    factor_ref,
-    table_hbm,
-    out_ref,
-    table_ref,
-    high_later,
-    low_later,
-    factor_later,
-    spread_ref,
-    table_sem,
-):
+def keep_kernel(blocks, *refs):
+    start_ref, core_ref, most_ref, repeated_ref, rank_ref, code_ref, *refs = refs
+    slot_refs = by_block(refs[: 3 * blocks])
+    table_hbm, out_ref, *refs = refs[3 * blocks :]
+    later_refs = by_block(refs[: 3 * blocks])
+    table_ref, spread_ref, table_sem = refs[3 * blocks :]
     table_copy = pltpu.make_async_copy(table_hbm, table_ref, table_sem)
     table_copy.start()
-    rows = table_ref.shape[0]
-    tiles = rows // lanes
+    tiles = table_ref.shape[0] // lanes
     core = core_ref[0]
-    slot_refs = (high_ref, low_ref, factor_ref)
-    later_refs = (high_later, low_later, factor_later)
     spread_half(slot_refs, spread_ref, core, tiles, False)
     rounds = rounds_for(most_ref[...])
 
@@ -294,66 +265,66 @@
     rows, width = table_rows.shape
     bag, batch = weight.shape
     padded = bag + 8 - bag % 8
-    groups = batch * slots // lanes
     half = batch // 2
     tiles = rows // lanes
+    blocks = batch // lanes
     smem = pl.BlockSpec(memory_space=pltpu.SMEM)
     vmem = pl.BlockSpec(memory_space=pltpu.VMEM)
     far = pl.BlockSpec(memory_space=pl.ANY)
+    by_position = jax.ShapeDtypeStruct((padded, batch), jnp.float32)
+    slot_shapes = [(n, lanes) for n in (slots, lanes, slots)] * blocks
+    slot = [jax.ShapeDtypeStruct(shape, jnp.float32) for shape in slot_shapes]
+    later = [pltpu.VMEM(shape, jnp.float32) for shape in slot_shapes]
     table_scratch = pltpu.VMEM((rows, width), table_rows.dtype)
-    by_position = jax.ShapeDtypeStruct((padded, batch), jnp.float32)
-    by_group = [pltpu.VMEM((n, lanes), jnp.float32) for n in (groups, lanes, groups)]
     spread = pltpu.VMEM(((half + 1) * tiles, lanes), jnp.float32)
     dma = pltpu.SemaphoreType.DMA
-    scratch = [
-        table_scratch,
-        pltpu.VMEM(index_rows.shape, index_rows.dtype),
-        pltpu.VMEM(weight.shape, weight.dtype),
-        pltpu.VMEM(length.shape, length.dtype),
-        *by_group,
-        spread,
-        dma,
-        dma,
-        dma,
-        dma,
-    ]
     limit = pltpu.CompilerParams(vmem_limit_bytes=vmem_bytes)
     index_rows, weight, length, table_rows = [
         pltpu.with_memory_space_constraint(value, pltpu.HBM)
         for value in (index_rows, weight, length, table_rows)
     ]
     pools = jax.ShapeDtypeStruct((half, width), jnp.float32)
-    slot = [jax.ShapeDtypeStruct((n, lanes), jnp.float32) for n in (groups, lanes, groups)]
     place = (row_start.reshape(1), core.reshape(1))
 
-    sent, high, low, factor, most, repeated, rank, code = pl.pallas_call(
-        send_kernel,
+    sent, most, repeated, rank, code, *slot_values = pl.pallas_call(
+        functools.partial(send_kernel, blocks),
         out_shape=(
             pools,
-            *slot,
             jax.ShapeDtypeStruct((8, lanes), jnp.float32),
             jax.ShapeDtypeStruct((tiles // 2, lanes), jnp.float32),
             by_position,
             by_position,
+            *slot,
         ),
         in_specs=[smem, smem, far, far, far, far],
-        out_specs=(vmem,) * 8,
-        scratch_shapes=scratch,
+        out_specs=(vmem,) * (5 + len(slot)),
+        scratch_shapes=[
+            *later,
+            pltpu.VMEM(index_rows.shape, index_rows.dtype),
+            pltpu.VMEM(weight.shape, weight.dtype),
+            pltpu.VMEM(length.shape, length.dtype),
+            table_scratch,
+            spread,
+            dma,
+            dma,
+            dma,
+            dma,
+        ],
         compiler_params=limit,
     )(*place, index_rows, weight, length, table_rows)
 
     def keep():
         return pl.pallas_call(
-            keep_kernel,
+            functools.partial(keep_kernel, blocks),
             out_shape=pools,
-            in_specs=[smem, smem, vmem, vmem, vmem, vmem, vmem, vmem, vmem, far],
+            in_specs=[smem, smem, *[vmem] * (4 + len(slot)), far],
             out_specs=vmem,
-            scratch_shapes=[table_scratch, *by_group, spread, dma],
+            scratch_shapes=[*later, table_scratch, spread, dma],
             compiler_params=limit,
             cost_estimate=pl.CostEstimate(
                 flops=8 * half * rows * width, bytes_accessed=rows * width * 2, transcendentals=0
             ),
-        )(*place, most, repeated, rank, code, high, low, factor, table_rows)
+        )(*place, most, repeated, rank, code, *slot_values, table_rows)
 
     return sent, keep
 

time: 31.5 us -> 32.5 us (1.032)
  Pallas kernels: 7.92 us -> 9.55 us
  blocking collectives: 19.2 us -> 18.8 us
  starting transfers between devices: 3.62 us -> 3.29 us
    pallas_call x2, Pallas kernels: 7.92 us -> 9.55 us  [the longest x1 6.05 us: kernels(): pl.pallas_call(functools.partial(send_kernel, blocks), out_shape=(pools,...]
    all_to_all x1, blocking collectives: 19.2 us -> 18.8 us  [on_device(): lax.all_to_all(tiles, ('table', 'pair', 'core'), split_axis=0, concat_axi...]
    ppermute x1, starting transfers between devices: 3.62 us -> 3.29 us  [on_device(): received = lax.ppermute(sent, 'core', [(0, 1), (1, 0)])]
  transfers between devices with their start and end apart: 1 -> 1, of which waited for: 0 -> 0; matrix products, arithmetic and copies ran while one was open for 0% -> 0% of each run, Pallas kernels for 10% -> 11%
where the time goes in v2:
time: 32.5 us; the launch traced here: 32.3 us
  blocking collectives  18.8 us (58%)
  Pallas kernels  9.55 us (29%)
  starting transfers between devices  3.29 us (10%)
  other arithmetic  0.64 us (2%)
    all_to_all x1, blocking collectives, on_device(): lax.all_to_all(tiles, ('table', 'pair', 'core'), split_axis=0, concat_axi...  18.8 us
    pallas_call x1, Pallas kernels, kernels(): pl.pallas_call(functools.partial(send_kernel, blocks), out_shape=(pools,...  6.05 us
    pallas_call x1, Pallas kernels, keep(): pl.pallas_call(functools.partial(keep_kernel, blocks), out_shape=pools, i...  3.5 us
    ppermute x1, starting transfers between devices, on_device(): received = lax.ppermute(sent, 'core', [(0, 1), (1, 0)])  3.29 us
  transfers between devices with their start and end apart: 1, of which 0 were waited for; matrix products, arithmetic and copies ran while one was open for 0% of the time, Pallas kernels for 11%

profile of v2, /device:TPU:1, one launch (start us, length us, event | category | flops | bytes accessed | tf_op | source)
XLA Modules:
  0.0 32.3 jit_solution(15939280232700887695)
XLA Ops:
  0.0 6.0 %shard_map.46 = (f32[256,128]{1,0:T(8,128)S(1)}, f32[8,128]{1,0:T(8,128)S(1)}, f32[32,128]{1,0:T(8,128)S(1)}, f32[104,512]{1,0:T(8,128)S(1)}, f32[104,512]{1,0:T...) custom-call(s32[1]{0:T(128)} %bitcast.refs_0_, ...), custom_call_target="tpu_custom_call" | custom-call | tf_op jit(solution)/shard_map/pallas_call | solution.py:289
  6.1 3.3 %collective-permute-start = (f32[256,128]{1,0:T(8,128)S(1)}, f32[256,128]{1,0:T(8,128)S(1)}, u32[]{:S(2)}, u32[]{:S(2)}) collective-permute-start(f32[256,128]{1,0:T(8,128)S(1)} %get-tuple-element.38), channel_id=1, source_target_pairs={{0,1},{1,0},{2,3},{3,2},{4,5},{5,4},{6,7},{7,6},{8,9},{9,8},{10,11... | collective-permute-start | bytes 393224 | tf_op jit(solution)/shard_map/ppermute | solution.py:341
  9.3 3.5 %shard_map.47 = f32[256,128]{1,0:T(8,128)S(1)} custom-call(s32[1]{0:T(128)} %bitcast.refs_0_, s32[1]{0:T(128)} %bitcast.1.refs_1_, f32[8,128]{1,0:T(8,128)S(1)} %get-tuple-element.22.refs_2_, f32[32,128]{1,0:T(8,128)S(1)} %get-tuple-element.23.refs_3_, f32[104,512]{1,0:T(8,128)S(1)} %get-tuple-element.24.refs_4_, f32[104,512]{1,0:T(8,128)S(1)} %get-tuple-element.25.refs_5_, ...), custom_call_target="tpu_custom_call" | custom-call | flops 2147483648 | bytes 2097152 | tf_op jit(solution)/shard_map/pallas_call | solution.py:317
  12.9 0.0 collective-permute-done
  12.9 18.8 %all_to_all.5 = f32[128,2,128]{2,1,0:T(2,128)S(1)} all-to-all(f32[128,2,128]{2,1,0:T(2,128)S(1)} %bitcast.10), channel_id=1, replica_groups={{52,54,48,50,60,62,56,58,36,38,32,34,44,46,40,42,20,22,16,18,28,30,24,2..., dimensions={0} | all-to-all | bytes 262144 | tf_op jit(solution)/shard_map/all_to_all | solution.py:349
  31.7 0.6 %bitcast_reduce_fusion = bf16[4,2,128]{2,1,0:T(2,128)(2,1)} fusion(f32[128,2,128]{2,1,0:T(2,128)S(1)} %all_to_all.5), kind=kLoop, calls=%fused_computation | loop fusion | flops 31744 | bytes 133120 | tf_op jit(solution)/shard_map/reduce_sum | solution.py:358
  (1 shorter events, 0.0 us)
Async XLA Ops:
  6.1 6.8 %collective-permute-start = (f32[256,128]{1,0:T(8,128)S(1)}, f32[256,128]{1,0:T(8,128)S(1)}, u32[]{:S(2)}, u32[]{:S(2)}) collective-permute-start(f32[256,128]{1,0:T(8,128)S(1)} %get-tuple-element.38), channel_id=1, source_target_pairs={{0,1},{1,0},{2,3},{3,2},{4,5},{5,4},{6,7},{7,6},{8,9},{9,8},{10,11... | collective-permute-start | bytes 393224 | tf_op jit(solution)/shard_map/ppermute | solution.py:341

commit v3 on v0

--- a/solution.py
+++ b/solution.py
@@ -73,7 +73,7 @@
         repeated_ref[where, :] = jnp.maximum(repeated_ref[where, :], any_in_pair(noted, pair))
 
 
-def fill_slots(rank_ref, code_ref, slot_refs, first, note=None, repeated_ref=None):
+def fill_slots(rank_ref, code_ref, slot_refs, first):
     high_ref, low_ref, factor_ref = slot_refs
     groups = high_ref.shape[0]
     planes = []
@@ -84,16 +84,15 @@
         for s in range(slots):
             at = rank == (first + s).astype(jnp.float32)
             planes.append(jnp.sum(jnp.where(at, code, 0.0), axis=0, keepdims=True))
-    plane = jnp.concatenate(planes, 0)
-    if note is not None:
-        note(plane, repeated_ref)
-    plane = jnp.concatenate([plane, pltpu.roll(plane, lanes - groups, 1)], 0)
+    slot_codes = jnp.concatenate(planes, 0)
+    plane = jnp.concatenate([slot_codes, pltpu.roll(slot_codes, lanes - groups, 1)], 0)
     low_ref[...] = (plane.astype(jnp.int32) // (2 * weight_unit) % lanes).astype(jnp.float32)
     code = plane.T[:groups].astype(jnp.int32)
     row = code // (2 * weight_unit)
     high_ref[...] = (row // lanes).astype(jnp.float32)
     factor = (code % (2 * weight_unit)).astype(jnp.float32)
     factor_ref[...] = factor * (1.0 / weight_unit)
+    return slot_codes
 
 
 def spread_half(slot_refs, spread_ref, core, tiles, add):
@@ -164,7 +163,9 @@
     left = [
         jnp.where(ours, repeated_ref[pair : pair + 1, :], 0.0) for pair in range(tiles // 2)
     ]
-    any_left = jnp.max(functools.reduce(jnp.maximum, left)) > 0
+    left_in_four = [
+        jnp.max(functools.reduce(jnp.maximum, left[i : i + 4])) > 0 for i in range(0, len(left), 4)
+    ]
     left = [jnp.max(some) > 0 for some in left]
     factors = [
         spread_ref[pl.ds(i * stride, bags), :].astype(jnp.bfloat16) for i in range(tiles)
@@ -183,10 +184,12 @@
             preferred_element_type=jnp.float32,
         )
 
-    @pl.when(any_left)
-    def _():
-        for pair in range(tiles // 2):
-            pl.when(left[pair])(functools.partial(add_rest, pair))
+    for four in range(tiles // 8):
+
+        @pl.when(left_in_four[four])
+        def _(four=four):
+            for pair in range(4 * four, 4 * four + 4):
+                pl.when(left[pair])(functools.partial(add_rest, pair))
 
 
 def send_kernel(
@@ -238,11 +241,12 @@
     rounds = rounds_for(most)
     slot_refs = (high_ref, low_ref, factor_ref)
     later_refs = (high_later, low_later, factor_later)
-    fill_slots(rank_ref, code_ref, slot_refs, jnp.int32(0), note_repeats, repeated_ref)
+    plane = fill_slots(rank_ref, code_ref, slot_refs, jnp.int32(0))
     spread_half(slot_refs, spread_ref, core, tiles, False)
+    note_repeats(plane, repeated_ref)
 
     def later_round(number, carry):
-        fill_slots(rank_ref, code_ref, later_refs, number * slots, note_later, repeated_ref)
+        note_later(fill_slots(rank_ref, code_ref, later_refs, number * slots), repeated_ref)
         spread_half(later_refs, spread_ref, core, tiles, True)
         return carry
 

time: 31.5 us -> 31.4 us (level)
  blocking collectives: 19.2 us -> 19.8 us
  starting transfers between devices: 3.62 us -> 3.29 us
    all_to_all x1, blocking collectives: 19.2 us -> 19.8 us  [on_device(): lax.all_to_all(tiles, ('table', 'pair', 'core'), split_axis=0, concat_axi...]
    ppermute x1, starting transfers between devices: 3.62 us -> 3.29 us  [on_device(): received = lax.ppermute(sent, 'core', [(0, 1), (1, 0)])]
  transfers between devices with their start and end apart: 1 -> 1, of which waited for: 0 -> 0; matrix products, arithmetic and copies ran while one was open for 0% -> 0% of each run, Pallas kernels for 10% -> 9%
where the time goes in v3:
time: 31.4 us; the launch traced here: 31.5 us
  blocking collectives  19.8 us (63%)
  Pallas kernels  7.66 us (24%)
  starting transfers between devices  3.29 us (10%)
  other arithmetic  0.64 us (2%)
    all_to_all x1, blocking collectives, on_device(): lax.all_to_all(tiles, ('table', 'pair', 'core'), split_axis=0, concat_axi...  19.8 us
    pallas_call x1, Pallas kernels, kernels(): pl.pallas_call(send_kernel, out_shape=(pools, *slot, jax.ShapeDtypeStruct...  4.73 us
    ppermute x1, starting transfers between devices, on_device(): received = lax.ppermute(sent, 'core', [(0, 1), (1, 0)])  3.29 us
    pallas_call x1, Pallas kernels, keep(): pl.pallas_call(keep_kernel, out_shape=pools, in_specs=[smem, smem, vmem,...  2.93 us
  transfers between devices with their start and end apart: 1, of which 0 were waited for; matrix products, arithmetic and copies ran while one was open for 0% of the time, Pallas kernels for 9%

profile of v3, /device:TPU:1, one launch (start us, length us, event | category | flops | bytes accessed | tf_op | source)
XLA Modules:
  0.0 31.5 jit_solution(17797781771526287902)
XLA Ops:
  0.0 4.7 %shard_map.46 = (f32[256,128]{1,0:T(8,128)S(1)}, f32[64,128]{1,0:T(8,128)S(1)}, f32[128,128]{1,0:T(8,128)S(1)}, f32[64,128]{1,0:T(8,128)S(1)}, f32[8,128]{1,0:T(...) custom-call(s32[1]{0:T(128)} %bitcast.start_ref, s32[1]{0:T(128)} %bitcast.1.core_ref, ...), custom_call_target="tpu_custom_call" | custom-call | tf_op jit(solution)/shard_map/pallas_call | solution.py:333
  4.7 3.3 %collective-permute-start = (f32[256,128]{1,0:T(8,128)S(1)}, f32[256,128]{1,0:T(8,128)S(1)}, u32[]{:S(2)}, u32[]{:S(2)}) collective-permute-start(f32[256,128]{1,0:T(8,128)S(1)} %get-tuple-element.20), channel_id=1, source_target_pairs={{0,1},{1,0},{2,3},{3,2},{4,5},{5,4},{6,7},{7,6},{8,9},{9,8},{10,11... | collective-permute-start | bytes 393224 | tf_op jit(solution)/shard_map/ppermute | solution.py:374
  8.0 2.9 %shard_map.47 = f32[256,128]{1,0:T(8,128)S(1)} custom-call(s32[1]{0:T(128)} %bitcast.start_ref, s32[1]{0:T(128)} %bitcast.1.core_ref, f32[8,128]{1,0:T(8,128)S(1)} %get-tuple-element.13.most_ref, f32[32,128]{1,0:T(8,128)S(1)} %get-tuple-element.14.repeated_ref, f32[104,512]{1,0:T(8,128)S(1)} %get-tuple-element.15.rank_ref, ...), custom_call_target="tpu_custom_call" | custom-call | flops 2147483648 | bytes 2097152 | tf_op jit(solution)/shard_map/pallas_call | solution.py:350
  11.0 0.0 collective-permute-done
  11.0 19.8 %all_to_all.5 = f32[128,2,128]{2,1,0:T(2,128)S(1)} all-to-all(f32[128,2,128]{2,1,0:T(2,128)S(1)} %bitcast.10), channel_id=1, replica_groups={{52,54,48,50,60,62,56,58,36,38,32,34,44,46,40,42,20,22,16,18,28,30,24,2..., dimensions={0} | all-to-all | bytes 262144 | tf_op jit(solution)/shard_map/all_to_all | solution.py:382
  30.8 0.6 %bitcast_reduce_fusion = bf16[4,2,128]{2,1,0:T(2,128)(2,1)} fusion(f32[128,2,128]{2,1,0:T(2,128)S(1)} %all_to_all.5), kind=kLoop, calls=%fused_computation | loop fusion | flops 31744 | bytes 133120 | tf_op jit(solution)/shard_map/reduce_sum | solution.py:391
  (1 shorter events, 0.0 us)
Async XLA Ops:
  4.7 6.2 %collective-permute-start = (f32[256,128]{1,0:T(8,128)S(1)}, f32[256,128]{1,0:T(8,128)S(1)}, u32[]{:S(2)}, u32[]{:S(2)}) collective-permute-start(f32[256,128]{1,0:T(8,128)S(1)} %get-tuple-element.20), channel_id=1, source_target_pairs={{0,1},{1,0},{2,3},{3,2},{4,5},{5,4},{6,7},{7,6},{8,9},{9,8},{10,11... | collective-permute-start | bytes 393224 | tf_op jit(solution)/shard_map/ppermute | solution.py:374

commit v4 on v3

--- a/solution.py
+++ b/solution.py
@@ -220,8 +220,16 @@
     weight_sem,
     length_sem,
 ):
+    half_bag = index_ref.shape[0] // 2
     copies = [
-        pltpu.make_async_copy(index_hbm, index_ref, index_sem),
+        *[
+            pltpu.make_async_copy(
+                index_hbm.at[pl.ds(part * half_bag, half_bag)],
+                index_ref.at[pl.ds(part * half_bag, half_bag)],
+                index_sem.at[part],
+            )
+            for part in range(2)
+        ],
         pltpu.make_async_copy(weight_hbm, weight_ref, weight_sem),
         pltpu.make_async_copy(length_hbm, length_ref, length_sem),
     ]
@@ -317,7 +325,7 @@
         *by_group,
         spread,
         dma,
-        dma,
+        dma((2,)),
         dma,
         dma,
     ]

time: 31.4 us -> 31.4 us (level); the launches traced: 31.5 us -> 31.1 us
    all_to_all x1, blocking collectives: 19.8 us -> 19.5 us  [on_device(): lax.all_to_all(tiles, ('table', 'pair', 'core'), split_axis=0, concat_axi...]
where the time goes in v4:
time: 31.4 us; the launch traced here: 31.1 us
  blocking collectives  19.5 us (62%)
  Pallas kernels  7.67 us (24%)
  starting transfers between devices  3.29 us (10%)
  other arithmetic  0.64 us (2%)
    all_to_all x1, blocking collectives, on_device(): lax.all_to_all(tiles, ('table', 'pair', 'core'), split_axis=0, concat_axi...  19.5 us
    pallas_call x1, Pallas kernels, kernels(): pl.pallas_call(send_kernel, out_shape=(pools, *slot, jax.ShapeDtypeStruct...  4.74 us
    ppermute x1, starting transfers between devices, on_device(): received = lax.ppermute(sent, 'core', [(0, 1), (1, 0)])  3.29 us
    pallas_call x1, Pallas kernels, keep(): pl.pallas_call(keep_kernel, out_shape=pools, in_specs=[smem, smem, vmem,...  2.93 us
  transfers between devices with their start and end apart: 1, of which 0 were waited for; matrix products, arithmetic and copies ran while one was open for 0% of the time, Pallas kernels for 9%

profile of v4, /device:TPU:1, one launch (start us, length us, event | category | flops | bytes accessed | tf_op | source)
XLA Modules:
  0.0 31.1 jit_solution(11420617293612559508)
XLA Ops:
  0.0 4.7 %shard_map.46 = (f32[256,128]{1,0:T(8,128)S(1)}, f32[64,128]{1,0:T(8,128)S(1)}, f32[128,128]{1,0:T(8,128)S(1)}, f32[64,128]{1,0:T(8,128)S(1)}, f32[8,128]{1,0:T(...) custom-call(s32[1]{0:T(128)} %bitcast.start_ref, s32[1]{0:T(128)} %bitcast.1.core_ref, ...), custom_call_target="tpu_custom_call" | custom-call | tf_op jit(solution)/shard_map/pallas_call | solution.py:341
  4.8 3.3 %collective-permute-start = (f32[256,128]{1,0:T(8,128)S(1)}, f32[256,128]{1,0:T(8,128)S(1)}, u32[]{:S(2)}, u32[]{:S(2)}) collective-permute-start(f32[256,128]{1,0:T(8,128)S(1)} %get-tuple-element.20), channel_id=1, source_target_pairs={{0,1},{1,0},{2,3},{3,2},{4,5},{5,4},{6,7},{7,6},{8,9},{9,8},{10,11... | collective-permute-start | bytes 393224 | tf_op jit(solution)/shard_map/ppermute | solution.py:382
  8.0 2.9 %shard_map.47 = f32[256,128]{1,0:T(8,128)S(1)} custom-call(s32[1]{0:T(128)} %bitcast.start_ref, s32[1]{0:T(128)} %bitcast.1.core_ref, f32[8,128]{1,0:T(8,128)S(1)} %get-tuple-element.13.most_ref, f32[32,128]{1,0:T(8,128)S(1)} %get-tuple-element.14.repeated_ref, f32[104,512]{1,0:T(8,128)S(1)} %get-tuple-element.15.rank_ref, ...), custom_call_target="tpu_custom_call" | custom-call | flops 2147483648 | bytes 2097152 | tf_op jit(solution)/shard_map/pallas_call | solution.py:358
  11.0 0.0 collective-permute-done
  11.0 19.5 %all_to_all.5 = f32[128,2,128]{2,1,0:T(2,128)S(1)} all-to-all(f32[128,2,128]{2,1,0:T(2,128)S(1)} %bitcast.10), channel_id=1, replica_groups={{52,54,48,50,60,62,56,58,36,38,32,34,44,46,40,42,20,22,16,18,28,30,24,2..., dimensions={0} | all-to-all | bytes 262144 | tf_op jit(solution)/shard_map/all_to_all | solution.py:390
  30.5 0.6 %bitcast_reduce_fusion = bf16[4,2,128]{2,1,0:T(2,128)(2,1)} fusion(f32[128,2,128]{2,1,0:T(2,128)S(1)} %all_to_all.5), kind=kLoop, calls=%fused_computation | loop fusion | flops 31744 | bytes 133120 | tf_op jit(solution)/shard_map/reduce_sum | solution.py:399
  (1 shorter events, 0.0 us)
Async XLA Ops:
  4.8 6.2 %collective-permute-start = (f32[256,128]{1,0:T(8,128)S(1)}, f32[256,128]{1,0:T(8,128)S(1)}, u32[]{:S(2)}, u32[]{:S(2)}) collective-permute-start(f32[256,128]{1,0:T(8,128)S(1)} %get-tuple-element.20), channel_id=1, source_target_pairs={{0,1},{1,0},{2,3},{3,2},{4,5},{5,4},{6,7},{7,6},{8,9},{9,8},{10,11... | collective-permute-start | bytes 393224 | tf_op jit(solution)/shard_map/ppermute | solution.py:382
